TPU v7x, 1024 devices: a whole 4x4x32 slice. The times are simulated.
1024 devices in a mesh: dp: 32 (over z_lo, x), expert: 32 (over z_hi, y, core).
Axes of the slice: x: 4, y: 4, z: 32 (z_hi: 4, z_lo: 8; z = z_hi * 8 + z_lo), core: 2. Of those that a mesh axis runs over, the one named last changes fastest.
Arguments:
- hidden: bfloat16 [131072, 1024], P(('dp', 'expert')), may hold values from -6 to 6
- grad_out: bfloat16 [131072, 1024], P(('dp', 'expert')), may hold values from -48 to 48
- router_weight: float32 [1024, 32], replicated, may hold values from -0.1875 to 0.1875
- expert_ids: int32 [131072, 6], P(('dp', 'expert')), may hold values from 0 to 31, all different within a row; in each aligned block of 64 rows (0 to 63, 64 to 127, ...) at most 13 rows name the same one
- pre_gate: bfloat16 [32, 32, 832, 704], P('dp', 'expert'), may hold values from -6 to 6
- pre_up: bfloat16 [32, 32, 832, 704], P('dp', 'expert'), may hold values from -6 to 6
- w_gate: bfloat16 [32, 1024, 704], P('expert'), may hold values from -0.1875 to 0.1875
- w_up: bfloat16 [32, 1024, 704], P('expert'), may hold values from -0.1875 to 0.1875
- w_down: bfloat16 [32, 704, 1024], P('expert'), may hold values from -0.21875 to 0.21875
Outputs:
- grad_x: bfloat16 [131072, 1024], P(('dp', 'expert'))
- router_update: float32 [1024, 32], P('dp', 'expert')
Inputs may be any that keep to these rules, and one draw needn't show every extreme that they name: `expert_ids`: each row names 6 different experts; in each aligned block of 64 rows no expert is named by more than 13 rows.
All inputs are finite; a program needn't handle non-finite values.
Results may differ from a plain program's by a relative error of at most 0.006.
Values may be sent and summed in bfloat16 or wider, within the bound.
A program may use at most 32 MiB of HBM per device.

v0:
```python
import jax
import jax.numpy as jnp
from jax import lax
from jax.sharding import Mesh
from jax.sharding import PartitionSpec as P

BLK = 64
EXPERT = ("expert_0", "expert_1", "expert_2")
DP = ("dp_0", "dp_1")
DP_EXPERT = ("dp_0", "dp_1", "expert_0", "expert_1", "expert_2")


PRECISE = lax.Precision.HIGHEST


def sent_together(arrays, axis, split_dim, concat_dim, along):
    columns = [a.reshape(*a.shape[:along], -1) for a in arrays]
    both = jnp.concatenate(columns, axis=along)
    out, at, finished = (
        lax.all_to_all(both, axis, split_axis=split_dim, concat_axis=concat_dim, tiled=True),
        0,
        [],
    )
    for a, column in zip(arrays, columns):
        piece = out[..., at : at + column.shape[along]]
        finished.append(piece.reshape(*piece.shape[:along], *a.shape[along:]))
        at += column.shape[along]
    return tuple(finished)


def cut_along(value, dim, size):
    dims = value.shape
    parts = value.reshape(*dims[:dim], size, dims[dim] // size, *dims[dim + 1 :])
    return jnp.moveaxis(parts, dim, 0)


def sent_and_summed(value, axis, dim):
    size = lax.axis_size(axis)
    parts = lax.all_to_all(cut_along(value, dim, size), axis, 0, 0, tiled=True)
    return jnp.sum(parts, axis=0)


def over_axes(value, axes):
    for axis in axes:
        value = lax.psum(value, axis)
    return value


def contract_last(left, right):
    return lax.dot_general(
        left, right, (((1,), (1,)), ((), ())), preferred_element_type=jnp.float32
    )


def slot_places(group_ids, block_rows, experts, capacity):
    tokens, top = group_ids.shape
    grouped = group_ids.reshape(tokens // block_rows, block_rows * top)
    hit_marks = (grouped[..., None] == jnp.arange(experts, dtype=jnp.int32)).astype(jnp.int32)
    earlier = jnp.cumsum(hit_marks, axis=1) - hit_marks
    slot_index = jnp.sum(earlier * hit_marks, axis=-1)
    flat_place = grouped * capacity + slot_index
    places = (flat_place[..., None] == jnp.arange(experts * capacity, dtype=jnp.int32)).astype(
        jnp.float32
    )
    return places.reshape(tokens // block_rows, block_rows, top, experts, capacity)


def expert_backward(sent_rows, gate_values, saved_gate, saved_up, w_gate, w_up, w_down):
    model_width = sent_rows.shape[-1]
    flat_rows = sent_rows.reshape(-1, model_width)
    dh_raw = contract_last(flat_rows, w_down)
    pre_first = saved_gate.reshape(-1, saved_gate.shape[-1]).astype(jnp.float32)
    pre_second = saved_up.reshape(-1, saved_up.shape[-1]).astype(jnp.float32)
    sigmoid_value = jax.nn.sigmoid(pre_first)
    active = pre_first * sigmoid_value
    slope_value = sigmoid_value * (1.0 + pre_first * (1.0 - sigmoid_value))
    gate_grad = jnp.sum(dh_raw * active * pre_second, axis=-1)
    dh_scaled = gate_values.reshape(-1, 1).astype(jnp.float32) * dh_raw
    d_first = (dh_scaled * pre_second * slope_value).astype(jnp.bfloat16)
    d_second = (dh_scaled * active).astype(jnp.bfloat16)
    back_rows = contract_last(d_first, w_gate) + contract_last(d_second, w_up)
    return (
        back_rows.astype(jnp.bfloat16).reshape(sent_rows.shape),
        gate_grad.astype(jnp.bfloat16).reshape(sent_rows.shape[:-1]),
    )


def local(hidden, grad_out, router_weight, expert_ids, pre_gate, pre_up, w_gate, w_up, w_down):
    tokens, model_width = hidden.shape
    experts = router_weight.shape[1]
    block_count = tokens // BLK
    senders = lax.axis_size(EXPERT)
    capacity = pre_gate.shape[2] // (block_count * senders)
    places = slot_places(expert_ids, BLK, experts, capacity)
    chosen = jnp.sum(places, axis=2)
    logits = jnp.dot(hidden.astype(jnp.float32), router_weight, precision=PRECISE)
    exponent = jnp.exp(logits)
    probability = exponent / jnp.sum(exponent, axis=-1, keepdims=True)
    picked = (expert_ids[..., None] == jnp.arange(experts, dtype=jnp.int32)).astype(jnp.float32)
    gate_values = jnp.sum(picked * probability[:, None, :], axis=-1)
    sent_rows = jnp.einsum(
        "nbec,nbd->necd",
        chosen.astype(jnp.bfloat16),
        grad_out.reshape(block_count, BLK, model_width),
        preferred_element_type=jnp.float32,
    ).astype(jnp.bfloat16)
    sent_gate = jnp.einsum(
        "nbkec,nbk->nec", places, gate_values.reshape(block_count, BLK, -1), precision=PRECISE
    ).astype(jnp.bfloat16)
    saved_first = pre_gate.reshape(block_count, senders, capacity, pre_gate.shape[-1])
    saved_second = pre_up.reshape(block_count, senders, capacity, pre_up.shape[-1])
    gate_matrix = w_gate[0]
    up_matrix = w_up[0]
    down_matrix = w_down[0]
    arrived, arrived_gate = sent_together((sent_rows, sent_gate), EXPERT, 1, 1, 3)
    back_rows, gate_grad = expert_backward(
        arrived, arrived_gate, saved_first, saved_second, gate_matrix, up_matrix, down_matrix
    )
    returned, returned_gate = sent_together((back_rows, gate_grad), EXPERT, 1, 1, 3)
    moe_grad = jnp.einsum(
        "nbec,necd->nbd", chosen.astype(jnp.bfloat16), returned, preferred_element_type=jnp.float32
    ).reshape(tokens, model_width)
    token_gate_grad = jnp.einsum(
        "nbkec,nec->nbk", places, returned_gate.astype(jnp.float32), precision=PRECISE
    ).reshape(tokens, -1)
    prob_grad = jnp.sum(picked * token_gate_grad[..., None], axis=1)
    logit_grad = probability * (
        prob_grad - jnp.sum(probability * prob_grad, axis=-1, keepdims=True)
    )
    grad_x = (moe_grad + jnp.dot(logit_grad, router_weight.T, precision=PRECISE)).astype(
        jnp.bfloat16
    )
    router_term = jnp.dot(hidden.astype(jnp.float32).T, logit_grad, precision=PRECISE)
    row_share = sent_and_summed(router_term, DP, 0)
    router_share = sent_and_summed(row_share, EXPERT, 1)
    square_total = over_axes(jnp.sum(router_share * router_share), DP_EXPERT)
    factor = jnp.minimum(1.0, jnp.sqrt(model_width * experts / (square_total + 1e-06)))
    return (grad_x, router_share * factor)


def solution(mesh):
    torus = Mesh(
        mesh.devices.reshape(8, 4, 4, 4, 2), ("dp_0", "dp_1", "expert_0", "expert_1", "expert_2")
    )
    return jax.shard_map(
        local,
        mesh=torus,
        in_specs=(
            P(DP_EXPERT, None),
            P(DP_EXPERT, None),
            P(),
            P(DP_EXPERT, None),
            P(DP, EXPERT, None, None),
            P(DP, EXPERT, None, None),
            P(EXPERT, None, None),
            P(EXPERT, None, None),
            P(EXPERT, None, None),
        ),
        out_specs=(P(DP_EXPERT, None), P(DP, EXPERT)),
        check_vma=False,
    )
```

profile of v0, /device:TPU:1, one launch (start us, length us, event | category | flops | bytes accessed | tf_op | source)
XLA Modules:
  0.0 582.6 jit_solution(16760128672875945545)
XLA Ops:
  0.7 0.9 copy.86
  1.6 0.1 eq.63
  1.7 0.1 eq.59
  1.9 0.7 broadcast_multiply_fusion
  2.6 1.8 reduce-window.6
  4.3 0.1 slice.24
  4.4 0.1 copy.88
  4.5 0.1 fusion.37
  4.7 0.1 reduce_sum.93
  4.8 0.1 copy.85
  4.9 0.1 copy.91
  5.0 1.4 fusion.47
  6.4 0.5 copy-done.14
  6.9 0.7 select_reduce_fusion.1
  7.6 0.1 reshape.120
  7.7 0.4 fusion.4
  8.1 2.5 fusion.30
  10.7 0.3 copy.92
  11.0 0.6 convolution_convert_fusion
  11.6 0.2 pad_maximum_fusion.1
  11.8 1.5 copy.93
  13.3 207.5 %all_to_all.20 = bf16[2,32,13,1025]{3,0,2,1:T(2,128)(2,1)S(1)} all-to-all(bf16[2,32,13,1025]{3,0,2,1:T(2,128)(2,1)S(1)} %copy.93), channel_id=1, replica_groups=mesh['dp_0'=8,'dp_1'=4,'expert_0'=4,'expert_1'=4,'expert_2'=2] {'expert_..., dimensions={1} | all-to-all | bytes 3411200 | tf_op jit(solution)/shard_map/all_to_all | solution.py:20
  220.8 1.3 copy-done.1
  222.0 1.2 slice.27
  223.2 0.6 copy.96
  223.8 1.5 reshape.110
  225.3 1.1 slice.26
  226.4 0.2 copy.112
  226.6 0.1 copy.95
  226.7 0.2 reshape.116
  226.9 5.4 fusion.7
  232.4 2.2 fusion.16
  234.6 2.9 add_convert_fusion
  237.5 2.5 reshape.111
  240.0 1.6 convert_element_type.94
  241.6 1.3 pad_maximum_fusion
  243.0 2.0 copy.98
  245.1 192.4 %all_to_all.21 = bf16[2,32,13,1025]{3,0,2,1:T(2,128)(2,1)S(1)} all-to-all(bf16[2,32,13,1025]{3,0,2,1:T(2,128)(2,1)S(1)} %copy.98), channel_id=1, replica_groups=mesh['dp_0'=8,'dp_1'=4,'expert_0'=4,'expert_1'=4,'expert_2'=2] {'expert_..., dimensions={1} | all-to-all | bytes 3411200 | tf_op jit(solution)/shard_map/all_to_all | solution.py:20
  437.5 0.8 slice.29
  438.3 1.1 copy.100
  439.5 0.0 copy-done.9
  439.5 0.6 fusion
  440.1 0.1 mul.113
  440.2 1.2 convolution_bitcast_fusion
  441.4 1.0 reshape.114
  442.4 2.2 copy.131
  444.5 1.3 reshape.126
  445.8 24.5 %all_to_all.22 = f32[32,1,1024]{2,1,0:T(1,128)} all-to-all(f32[32,1,1024]{2,1,0:T(1,128)S(1)} %reshape.126), channel_id=1, replica_groups=mesh['dp_0'=8,'dp_1'=4,'expert_0'=4,'expert_1'=4,'expert_2'=2] {'dp_0','..., dimensions={0} | all-to-all | bytes 262144 | tf_op jit(solution)/shard_map/all_to_all | solution.py:39
  470.3 0.5 broadcast.63
  470.8 1.9 reduce.2
  472.7 1.0 reshape.127
  473.7 1.1 bitcast_reduce_fusion
  474.8 32.8 %all_to_all.23 = f32[32,32,1]{1,2,0:T(1,128)S(1)} all-to-all(f32[32,32,1]{1,2,0:T(1,128)S(1)} %bitcast.115), channel_id=1, replica_groups=mesh['dp_0'=8,'dp_1'=4,'expert_0'=4,'expert_1'=4,'expert_2'=2] {'expert_..., dimensions={0} | all-to-all | bytes 8192 | tf_op jit(solution)/shard_map/all_to_all | solution.py:39
  507.5 0.1 reduce_sum.101
  507.6 0.6 multiply_reduce_fusion.1
  508.2 24.3 %psum.35 = f32[]{:T(128)} all-reduce(f32[]{:T(128)} %multiply_reduce_fusion.1), channel_id=1, replica_groups=mesh['dp_0'=8,'dp_1'=4,'expert_0'=4,'expert_1'=4,'expert_2'=2] {'dp_0'}, use_global_device_ids=true, to_apply=%region_12.13 | all-reduce | flops 1 | bytes 8 | tf_op jit(solution)/shard_map/psum | solution.py:45
  532.4 7.7 %psum.36 = f32[]{:T(128)} all-reduce(f32[]{:T(128)} %psum.35), channel_id=1, replica_groups=mesh['dp_0'=8,'dp_1'=4,'expert_0'=4,'expert_1'=4,'expert_2'=2] {'dp_1'}, use_global_device_ids=true, to_apply=%region_13.14 | all-reduce | flops 1 | bytes 8 | tf_op jit(solution)/shard_map/psum | solution.py:45
  540.2 2.4 slice.28
  542.5 14.4 %psum.37 = f32[]{:T(128)} all-reduce(f32[]{:T(128)} %psum.36), channel_id=1, replica_groups=mesh['dp_0'=8,'dp_1'=4,'expert_0'=4,'expert_1'=4,'expert_2'=2] {'expert_0'}, use_global_device_ids=true, to_apply=%region_14.15 | all-reduce | flops 1 | bytes 8 | tf_op jit(solution)/shard_map/psum | solution.py:45
  557.0 2.3 fusion.13
  559.3 7.7 %psum.38 = f32[]{:T(128)} all-reduce(f32[]{:T(128)} %psum.37), channel_id=1, replica_groups=mesh['dp_0'=8,'dp_1'=4,'expert_0'=4,'expert_1'=4,'expert_2'=2] {'expert_1'}, use_global_device_ids=true, to_apply=%region_15.16 | all-reduce | flops 1 | bytes 8 | tf_op jit(solution)/shard_map/psum | solution.py:45
  567.0 1.3 fusion.29
  568.3 13.1 %psum.39 = f32[]{:T(128)} all-reduce(f32[]{:T(128)} %psum.38), channel_id=1, replica_groups=mesh['dp_0'=8,'dp_1'=4,'expert_0'=4,'expert_1'=4,'expert_2'=2] {'expert_2'}, use_global_device_ids=true, to_apply=%region_16.17 | all-reduce | flops 1 | bytes 8 | tf_op jit(solution)/shard_map/psum | solution.py:45
  582.1 0.5 multiply_bitcast_fusion
  (46 shorter events, 0.2 us)
Async XLA Ops:
  0.6 231.7 %copy-start = (bf16[1,1024,704]{1,2,0:T(8,128)(2,1)S(1)}, bf16[1,1024,704]{1,2,0:T(8,128)(2,1)}, u32[]{:S(2)}) copy-start(bf16[1,1024,704]{1,2,0:T(8,128)(2,1)} %param.15) | copy-start | bytes 4325380
  0.6 10.3 %copy-start.4 = (bf16[128,1024]{1,0:T(8,128)(2,1)S(1)}, bf16[128,1024]{1,0:T(8,128)(2,1)}, u32[]{:S(2)}) copy-start(bf16[128,1024]{1,0:T(8,128)(2,1)} %param.10) | copy-start | bytes 786436
  2.6 8.1 %copy-start.10 = (s32[32,13]{0,1:T(8,128)}, s32[32,13]{0,1:T(8,128)S(1)}, u32[]{:S(2)}) copy-start(s32[32,13]{0,1:T(8,128)S(1)} %multiply_add_fusion) | copy-start | bytes 4996
  5.0 5.7 copy-start.8
  6.4 0.5 copy-start.14
  6.4 5.4 copy-start.5
  8.1 3.7 copy-start.2
  220.8 1.3 copy-start.1
  226.9 5.4 copy-start.17
  226.9 5.4 copy-start.18
  232.4 2.2 copy-start.16
  245.0 194.4 %copy-start.9 = (s32[2,64,6]{1,2,0:T(8,128)S(1)}, s32[2,64,6]{1,2,0:T(8,128)}, u32[]{:S(2)}) copy-start(s32[2,64,6]{1,2,0:T(8,128)} %copy-done.8) | copy-start | bytes 9220
  245.0 194.4 %copy-start.11 = (s32[32,13]{0,1:T(8,128)S(1)}, s32[32,13]{0,1:T(8,128)}, u32[]{:S(2)}) copy-start(s32[32,13]{0,1:T(8,128)} %copy-done.10) | copy-start | bytes 4996
  245.1 195.1 %copy-start.7 = (s32[128,6]{0,1:T(8,128)S(1)}, s32[128,6]{0,1:T(8,128)}, u32[]{:S(2)}) copy-start(s32[128,6]{0,1:T(8,128)} %param.12) | copy-start | bytes 9220
  245.1 195.1 %copy-start.6 = (f32[128,32]{0,1:T(8,128)S(1)}, f32[128,32]{0,1:T(8,128)}, u32[]{:S(2)}) copy-start(f32[128,32]{0,1:T(8,128)} %copy-done.5) | copy-start | bytes 49156
  245.1 195.1 %copy-start.15 = (f32[128]{0:T(128)S(1)}, f32[128]{0:T(128)}, u32[]{:S(2)}) copy-start(f32[128]{0:T(128)} %copy-done.14) | copy-start | bytes 1540
  440.2 34.6 %copy-start.12 = (f32[128]{0:T(128)}, f32[128]{0:T(128)S(1)}, u32[]{:S(2)}) copy-start(f32[128]{0:T(128)S(1)} %multiply_reduce_fusion) | copy-start | bytes 1540
  540.2 26.8 %copy-start.3 = (f32[1024,32]{0,1:T(8,128)S(1)}, f32[1024,32]{0,1:T(8,128)}, u32[]{:S(2)}) copy-start(f32[1024,32]{0,1:T(8,128)} %param.11) | copy-start | bytes 393220
  540.2 26.8 %copy-start.13 = (f32[128]{0:T(128)S(1)}, f32[128]{0:T(128)}, u32[]{:S(2)}) copy-start(f32[128]{0:T(128)} %copy-done.12) | copy-start | bytes 1540
where the time goes:
time: 584 us; the launch traced here: 583 us
  blocking collectives  524 us (90%)
  local copies, waits for them, and re-layouts  26.8 us (5%)
  matrix products  20.4 us (3%)
  other arithmetic  9.41 us (2%)
    all_to_all x2, blocking collectives, sent_together(): lax.all_to_all(both, axis, split_axis=split_dim, concat_axis=concat_dim,...  400 us
    psum x5, blocking collectives, over_axes(): value = lax.psum(value, axis)  67.2 us
    all_to_all x2, blocking collectives, sent_and_summed(): parts = lax.all_to_all(cut_along(value, dim, size), axis, 0, 0, tiled=True)  57.3 us

commit v1 on v0

v1 whole, which is shorter than its diff:
```python
import jax
import jax.numpy as jnp
from jax import lax
from jax.experimental import pallas as pl
from jax.experimental.pallas import tpu as pltpu
from jax.sharding import Mesh
from jax.sharding import PartitionSpec as P

EXPERT = ("expert_0", "expert_1", "expert_2")
DP = ("dp_0", "dp_1")
DP_EXPERT = DP + EXPERT
PRECISE = lax.Precision.HIGHEST
F32 = jnp.float32
BF16 = jnp.bfloat16
WIDE = 1152


def dot(a, b, dims=((1,), (0,)), precision=None):
    return lax.dot_general(a, b, (dims, ((), ())), preferred_element_type=F32, precision=precision)


def iota(shape, dim):
    return lax.broadcasted_iota(jnp.int32, shape, dim)


def kernel(
    rows_ref, hidden_ref, rw_ref, rwt_ref, ids_ref, pre_gate_hbm, pre_up_hbm, wg_hbm, wu_hbm, wd_hbm,
    gx_ref, ru_ref,
    pre_gate, pre_up, wg, wu, wd, gathered, aux, aux_in, aux_relay,
    packed, arrived, back, returned, up_slope, act, act_up, probs,
    own_part, relay_part, comb_out, comb_mid, comb_in, pg_out, pg_relay, pg_all,
    terms, zl_in, stage_out, x_in, slab_in, zh_in, sq_out, sq_in, turned,
    local_sem, row_ss, row_rs, aux_ss, aux_rs, go_ss, go_rs, ret_ss, ret_rs,
    comb_ss, comb_rs, pg_ss, pg_rs, zl_ss, zl_rs, x_ss, x_rs, slab_ss, slab_rs, zh_ss, zh_rs, sq_ss, sq_rs,
):
    zl, x = lax.axis_index("dp_0"), lax.axis_index("dp_1")
    zh, y, c = (lax.axis_index(a) for a in EXPERT)
    yc = y * 2 + c
    up_z, down_z, far_z = lax.rem(zh + 1, 4), lax.rem(zh + 3, 4), lax.rem(zh + 2, 4)
    origin = (zh, down_z, up_z, far_z)
    sent = []

    def at_z(z):
        return {"expert_0": z}

    def at_slab(place):
        return {"expert_1": place // 2, "expert_2": lax.rem(place, 2)}

    def copy(src, dst, ss, rs, to):
        return pltpu.make_async_remote_copy(
            src_ref=src, dst_ref=dst, send_sem=ss, recv_sem=rs,
            device_id=to, device_id_type=pl.DeviceIdType.MESH,
        )

    def send(*args):
        made = copy(*args)
        made.start()
        sent.append(made)
        return made

    local = [
        pltpu.make_async_copy(src, dst, local_sem.at[i])
        for i, (src, dst) in enumerate(
            ((pre_gate_hbm, pre_gate), (pre_up_hbm, pre_up), (wd_hbm, wd), (wg_hbm, wg), (wu_hbm, wu))
        )
    ]
    for made in local:
        made.start()
    barrier = pltpu.get_barrier_semaphore()
    meet = [at_z(up_z), at_z(down_z)]
    meet += [at_slab(lax.rem(yc + d, 8)) for d in range(1, 8)]
    meet += [{"dp_0": lax.rem(zl + d, 8)} for d in range(1, 8)]
    meet += [{"dp_1": lax.rem(x + d, 4)} for d in range(1, 4)]
    for to in meet:
        pl.semaphore_signal(barrier, inc=1, device_id=to, device_id_type=pl.DeviceIdType.MESH)

    logits = dot(hidden_ref[...].astype(F32), rw_ref[...], precision=PRECISE)
    exponent = jnp.exp(logits.T[:32])
    probability = exponent / jnp.sum(exponent, axis=0, keepdims=True)
    probs[...] = probability
    ids = ids_ref[...]
    expert = iota((32, 128), 0)
    chosen = jnp.zeros((32, 128), F32)
    for k in range(6):
        chosen += jnp.where(expert == ids[k : k + 1], 1.0, 0.0)
    r, t = iota((128, 128), 0), iota((128, 128), 1)
    earlier = jnp.where((r < t) & ((r >> 6) == (t >> 6)), 1.0, 0.0).astype(BF16)
    slot = jnp.where(chosen > 0.5, dot(chosen.astype(BF16), earlier), -1.0)
    for b in range(4):
        aux[b] = jnp.concatenate([slot[8 * b : 8 * b + 8], probability[8 * b : 8 * b + 8]], axis=0).astype(BF16)
    pl.semaphore_wait(barrier, len(meet))

    first, last = pl.ds(0, 64), pl.ds(64, 64)
    z_up, z_down = at_z(up_z), at_z(down_z)
    r1 = send(rows_ref.at[first], gathered.at[0, first], row_ss.at[0], row_rs.at[0], z_up)
    l1 = send(rows_ref.at[last], gathered.at[1, last], row_ss.at[1], row_rs.at[1], z_down)
    a_up = send(aux.at[up_z], aux_in.at[0], aux_ss.at[0], aux_rs.at[0], z_up)
    a_down = send(aux.at[down_z], aux_in.at[1], aux_ss.at[1], aux_rs.at[1], z_down)
    a_far = send(aux.at[far_z], aux_relay, aux_ss.at[2], aux_rs.at[2], z_up)
    r2 = send(rows_ref.at[last], gathered.at[0, last], row_ss.at[2], row_rs.at[2], z_up)
    l2 = send(rows_ref.at[first], gathered.at[1, first], row_ss.at[3], row_rs.at[3], z_down)

    def places(info):
        at = jnp.broadcast_to(info[:8].reshape(8, 1, 128), (8, 32, 128)).reshape(256, 128)
        r, t = iota((256, 128), 0), iota((256, 128), 1)
        hit = (at == (r & 15).astype(F32)) & (((r >> 4) & 1) == (t >> 6))
        return jnp.where(hit, 1.0, 0.0)

    def info_of(k):
        return (aux[zh] if k == 0 else aux_in[k - 1]).astype(F32)

    mine = pl.ds(pl.multiple_of(yc * 32, 32), 32)

    def slab_send(k, src, dst, ss, rs):
        dst[k, mine] = src[k, mine]
        for d in range(1, 8):
            place = lax.rem(yc + d, 8)
            theirs = pl.ds(pl.multiple_of(place * 32, 32), 32)
            send(src.at[k, theirs], dst.at[k, mine], ss.at[k, d], rs.at[k, d], at_slab(place))

    def slab_wait(k, src, dst, ss, rs):
        for d in range(1, 8):
            place = lax.rem(yc + 8 - d, 8)
            theirs = pl.ds(pl.multiple_of(place * 32, 32), 32)
            copy(src.at[k, theirs], dst.at[k, theirs], ss.at[k, d], rs.at[k, d], at_slab(place)).wait_recv()

    def dispatch(k):
        rows = rows_ref[...] if k == 0 else gathered[k - 1]
        packed[k] = dot(places(info_of(k)).astype(BF16), rows).astype(BF16)
        slab_send(k, packed, arrived, go_ss, go_rs)

    def run_expert(k):
        slab_wait(k, packed, arrived, go_ss, go_rs)
        o = origin[k]
        dh = dot(arrived[k], wd[...], ((1,), (1,)))
        gate_grad = jnp.sum(dh * act_up[o], axis=1, keepdims=True)
        d_first = (dh * up_slope[o]).astype(BF16)
        d_second = (dh * act[o]).astype(BF16)
        rows = dot(d_first, wg[...], ((1,), (1,))) + dot(d_second, wu[...], ((1,), (1,)))
        back[k, :, :1024] = rows.astype(BF16)
        back[k, :, 1024:] = jnp.broadcast_to(gate_grad, (256, 128)).astype(BF16)
        slab_send(k, back, returned, ret_ss, ret_rs)

    def combine(k):
        slab_wait(k, back, returned, ret_ss, ret_rs)
        info = info_of(k)
        hit = places(info)
        gate = jnp.broadcast_to(info[8:].reshape(8, 1, 128), (8, 32, 128)).reshape(256, 128)
        weights = (hit * gate).T.astype(BF16)
        part = dot(weights, returned[k, :, :1024])
        gate_grad = hit * returned[k, :, 1024:].astype(F32)
        return part, jnp.sum(gate_grad.reshape(8, 32, 128), axis=1)

    dispatch(0)

    local[0].wait()
    local[1].wait()
    r, s = iota((256, 104), 0), iota((256, 104), 1)
    for o in range(4):
        gate_in, up_in = jnp.zeros((256, 704), F32), jnp.zeros((256, 704), F32)
        for n in range(2):
            real = (s == (r >> 5) * 13 + (r & 15)) & ((r & 15) < 13) & (((r >> 4) & 1) == n)
            spread = jnp.where(real, 1.0, 0.0).astype(BF16)
            gate_in += dot(spread, pre_gate[n * 4 + o])
            up_in += dot(spread, pre_up[n * 4 + o])
        sg = 1.0 / (1.0 + jnp.exp(-gate_in))
        active = gate_in * sg
        act[o] = active
        act_up[o] = active * up_in
        up_slope[o] = up_in * (sg * (1.0 + gate_in * (1.0 - sg)))
    for made in local[2:]:
        made.wait()
    run_expert(0)

    r1.wait_recv()
    r3 = send(gathered.at[0, first], gathered.at[2, first], row_ss.at[4], row_rs.at[4], z_up)
    l1.wait_recv()
    l3 = send(gathered.at[1, last], gathered.at[2, last], row_ss.at[5], row_rs.at[5], z_down)
    a_far.wait_recv()
    a_relay = send(aux_relay, aux_in.at[2], aux_ss.at[3], aux_rs.at[3], z_up)
    part, own_gate_grad = combine(0)
    own_part[...] = part
    pg_all[zh] = own_gate_grad

    a_up.wait_recv()
    r2.wait_recv()
    dispatch(1)
    a_down.wait_recv()
    l2.wait_recv()
    dispatch(2)
    run_expert(1)
    run_expert(2)
    part, gate_grad = combine(1)
    pg_out[0] = gate_grad
    p_down = send(pg_out.at[0], pg_all.at[zh], pg_ss.at[0], pg_rs.at[0], z_down)
    comb_out[0] = part[:64].astype(BF16)
    c_down = send(comb_out.at[0], comb_in.at[1, 0], comb_ss.at[0], comb_rs.at[0], z_down)
    relay_part[1] = part[64:]
    part, gate_grad = combine(2)
    pg_out[1] = gate_grad
    p_up = send(pg_out.at[1], pg_all.at[zh], pg_ss.at[1], pg_rs.at[1], z_up)
    comb_out[1] = part[64:].astype(BF16)
    c_up = send(comb_out.at[1], comb_in.at[0, 1], comb_ss.at[1], comb_rs.at[1], z_up)
    relay_part[0] = part[:64]

    a_relay.wait_recv()
    r3.wait_recv()
    l3.wait_recv()
    dispatch(3)
    run_expert(3)
    part, gate_grad = combine(3)
    pg_out[2] = gate_grad
    p_far = send(pg_out.at[2], pg_relay, pg_ss.at[2], pg_rs.at[2], z_up)
    comb_out[2] = part[:64].astype(BF16)
    comb_out[3] = part[64:].astype(BF16)
    f_up = send(comb_out.at[2], comb_mid.at[0], comb_ss.at[2], comb_rs.at[2], z_up)
    f_down = send(comb_out.at[3], comb_mid.at[1], comb_ss.at[3], comb_rs.at[3], z_down)
    p_far.wait_recv()
    p_relay = send(pg_relay, pg_all.at[down_z], pg_ss.at[3], pg_rs.at[3], z_up)

    p_down.wait_recv()
    p_up.wait_recv()
    p_relay.wait_recv()
    probability = probs[...]
    prob_grad = pg_all[...].reshape(32, 128)
    logit_grad = probability * (prob_grad - jnp.sum(probability * prob_grad, axis=0, keepdims=True))
    term = dot(logit_grad, hidden_ref[...].astype(F32), precision=PRECISE)
    for i in range(8):
        terms[i] = term[:, 128 * i : 128 * i + 128]

    def share(src, dst, ss, rs, me, count, to):
        made = []
        for d in range(1, count):
            place = lax.rem(me + d, count)
            made.append(send(src(place), dst.at[me], ss.at[d], rs.at[d], to(place)))
        return made

    def gather(src, dst, ss, rs, me, count, to):
        for d in range(1, count):
            place = lax.rem(me + count - d, count)
            copy(src(place), dst.at[place], ss.at[d], rs.at[d], to(place)).wait_recv()

    zl_args = (lambda place: terms.at[place], zl_in, zl_ss, zl_rs, zl, 8, lambda place: {"dp_0": place})
    x_args = (lambda place: stage_out.at[0], x_in, x_ss, x_rs, x, 4, lambda place: {"dp_1": place})
    slab_args = (lambda place: stage_out.at[1], slab_in, slab_ss, slab_rs, yc, 8, at_slab)
    sq_args = (lambda place: sq_out, sq_in, sq_ss, sq_rs, zl, 8, lambda place: {"dp_0": place})
    zl_in[zl] = terms[zl]
    share(*zl_args)

    f_up.wait_recv()
    comb_out[4] = (relay_part[0] + comb_mid[0].astype(F32)).astype(BF16)
    e_up = send(comb_out.at[4], comb_in.at[0, 0], comb_ss.at[4], comb_rs.at[4], z_up)
    f_down.wait_recv()
    comb_out[5] = (relay_part[1] + comb_mid[1].astype(F32)).astype(BF16)
    e_down = send(comb_out.at[5], comb_in.at[1, 1], comb_ss.at[5], comb_rs.at[5], z_down)

    gather(*zl_args)
    total = jnp.sum(zl_in[...], axis=0)
    stage_out[0] = total
    x_in[x] = total
    share(*x_args)
    padded = jnp.concatenate([logit_grad, jnp.zeros((96, 128), F32)], axis=0).T
    own_part[...] += dot(padded, rwt_ref[...], precision=PRECISE)
    gather(*x_args)
    total = jnp.sum(x_in[...], axis=0)
    stage_out[1] = total
    slab_in[yc] = total
    share(*slab_args)
    gather(*slab_args)
    total = jnp.sum(slab_in[...], axis=0)
    stage_out[2] = total
    h1 = send(stage_out.at[2], zh_in.at[0], zh_ss.at[0], zh_rs.at[0], at_z(zh + 1 - 2 * lax.rem(zh, 2)))
    h1.wait_recv()
    total = total + zh_in[0]
    stage_out[3] = total
    h2 = send(stage_out.at[3], zh_in.at[1], zh_ss.at[1], zh_rs.at[1], at_z(3 - zh))
    h2.wait_recv()
    total = total + zh_in[1]
    square = jnp.sum(jnp.sum(total * total, axis=1, keepdims=True), axis=0, keepdims=True)
    square = jnp.broadcast_to(square, (8, 128))
    sq_out[...] = square
    sq_in[zl] = square
    share(*sq_args)

    c_down.wait_recv()
    c_up.wait_recv()
    e_up.wait_recv()
    e_down.wait_recv()
    for half in range(2):
        at = pl.ds(64 * half, 64)
        both = comb_in[0, half].astype(F32) + comb_in[1, half].astype(F32)
        gx_ref[at] = (own_part[at] + both).astype(BF16)

    turned[...] = jnp.concatenate([total, jnp.zeros((96, 128), F32)], axis=0).T
    column = turned[pl.ds(pl.multiple_of(x * 32, 32), 32)]
    column = jnp.where(iota((32, 128), 1) == zh * 8 + yc, column, 0.0)
    column = jnp.sum(column, axis=1, keepdims=True)
    gather(*sq_args)
    square = jnp.sum(sq_in[...], axis=0)[:1, :1]
    ru_ref[...] = column * jnp.minimum(1.0, jnp.sqrt(1024 * 32 / (square + 1e-06)))
    for made in sent:
        made.wait_send()


def local(hidden, grad_out, router_weight, expert_ids, pre_gate, pre_up, w_gate, w_up, w_down):
    vmem, dma = pltpu.VMEM, pltpu.SemaphoreType.DMA
    wide = jnp.pad(router_weight, ((0, 0), (0, 96)))
    ids = jnp.pad(expert_ids.T, ((0, 2), (0, 0)))
    in_vmem, in_hbm = pl.BlockSpec(memory_space=pltpu.VMEM), pl.BlockSpec(memory_space=pl.ANY)
    return pl.pallas_call(
        kernel,
        out_shape=(jax.ShapeDtypeStruct((128, 1024), BF16), jax.ShapeDtypeStruct((32, 1), F32)),
        in_specs=[in_vmem] * 5 + [in_hbm] * 5,
        out_specs=(in_vmem, in_vmem),
        scratch_shapes=[
            vmem((8, 104, 704), BF16), vmem((8, 104, 704), BF16),
            vmem((1024, 704), BF16), vmem((1024, 704), BF16), vmem((704, 1024), BF16),
            vmem((3, 128, 1024), BF16), vmem((4, 16, 128), BF16), vmem((3, 16, 128), BF16), vmem((16, 128), BF16),
            vmem((4, 256, 1024), BF16), vmem((4, 256, 1024), BF16), vmem((4, 256, WIDE), BF16), vmem((4, 256, WIDE), BF16),
            vmem((4, 256, 704), F32), vmem((4, 256, 704), F32), vmem((4, 256, 704), F32), vmem((32, 128), F32),
            vmem((128, 1024), F32), vmem((2, 64, 1024), F32), vmem((6, 64, 1024), BF16), vmem((2, 64, 1024), BF16),
            vmem((2, 2, 64, 1024), BF16), vmem((3, 8, 128), F32), vmem((8, 128), F32), vmem((4, 8, 128), F32),
            vmem((8, 32, 128), F32), vmem((8, 32, 128), F32), vmem((4, 32, 128), F32), vmem((4, 32, 128), F32),
            vmem((8, 32, 128), F32), vmem((2, 32, 128), F32), vmem((8, 128), F32), vmem((8, 8, 128), F32),
            vmem((128, 128), F32),
            dma((5,)), dma((6,)), dma((6,)), dma((4,)), dma((4,)), dma((4, 8)), dma((4, 8)), dma((4, 8)), dma((4, 8)),
            dma((6,)), dma((6,)), dma((4,)), dma((4,)), dma((8,)), dma((8,)), dma((4,)), dma((4,)), dma((8,)), dma((8,)),
            dma((2,)), dma((2,)), dma((8,)), dma((8,)),
        ],
        compiler_params=pltpu.CompilerParams(collective_id=0, has_side_effects=True),
    )(
        grad_out, hidden, wide, wide.T, ids,
        pre_gate.reshape(8, 104, 704), pre_up.reshape(8, 104, 704), w_gate[0], w_up[0], w_down[0],
    )


def solution(mesh):
    torus = Mesh(mesh.devices.reshape(8, 4, 4, 4, 2), DP_EXPERT)
    return jax.shard_map(
        local,
        mesh=torus,
        in_specs=(
            P(DP_EXPERT, None),
            P(DP_EXPERT, None),
            P(),
            P(DP_EXPERT, None),
            P(DP, EXPERT, None, None),
            P(DP, EXPERT, None, None),
            P(EXPERT, None, None),
            P(EXPERT, None, None),
            P(EXPERT, None, None),
        ),
        out_specs=(P(DP_EXPERT, None), P(DP, EXPERT)),
        check_vma=False,
    )
```

time: 584 us -> 233 us (0.40)
  blocking collectives: 524 us -> 0 us
  Pallas kernels: 0 us -> 217 us
  matrix products: 20.4 us -> 0 us
  local copies, waits for them, and re-layouts: 26.8 us -> 14.9 us
  other arithmetic: 9.41 us -> 0 us
    all_to_all x4 -> x0, blocking collectives: 457 us -> none  [the longest x2 400 us: sent_together(): lax.all_to_all(both, axis, split_axis=split_dim, concat_axis=concat_dim,...]
    pallas_call x0 -> x1, Pallas kernels: none -> 217 us  [local(): pl.pallas_call(kernel, out_shape=(jax.ShapeDtypeStruct((128, 1024), BF16)...]
    psum x5 -> x0, blocking collectives: 67.2 us -> none  [over_axes(): value = lax.psum(value, axis)]
    dot_general x10 -> x0, matrix products: 20.4 us -> none  [the longest x3 10.5 us: contract_last(): lax.dot_general(left, right, (((1,), (1,)), ((), ())), preferred_element_...]
    reshape x6 -> x0, local copies, waits for them, and re-layouts: 7.49 us -> none  [the longest x2 3.12 us: cut_along(): parts = value.reshape(*dims[:dim], size, dims[dim] // size, *dims[dim + 1:])]
    slice x8 -> x0, local copies, waits for them, and re-layouts: 7.37 us -> none  [the longest x6 7.17 us: sent_together(): piece = out[..., at:at + column.shape[along]]]
where the time goes in v1:
time: 233 us
  Pallas kernels  217 us (93%)
  local copies, waits for them, and re-layouts  14.9 us (6%)
    pallas_call x1, Pallas kernels, local(): pl.pallas_call(kernel, out_shape=(jax.ShapeDtypeStruct((128, 1024), BF16)...  217 us
    unnamed x14, local copies, waits for them, and re-layouts  9.65 us

profile of v1, /device:TPU:1, one launch (start us, length us, event | category | flops | bytes accessed | tf_op | source)
XLA Modules:
  0.0 232.5 jit_solution(13520748496489746680)
XLA Ops:
  0.6 0.0 copy-start.2
  0.6 1.4 pad.9.ids_ref
  2.0 1.7 pad_bitcast_fusion.rwt_ref
  3.8 1.1 copy.17
  4.9 0.8 pad.8.clone.rw_ref
  5.7 0.0 copy-done.2
  5.7 0.0 copy-start.3
  5.7 1.9 copy.11
  7.6 0.0 copy-start
  7.6 0.0 copy-done.3
  7.6 1.9 copy.12
  9.5 0.0 copy-done
  9.5 0.0 copy-start.1
  9.5 1.6 copy.13
  11.0 0.0 copy-done.1
  11.0 1.6 copy.14
  12.6 216.9 %shard_map.104 = (bf16[128,1024]{1,0:T(8,128)(2,1)}, f32[32,1]{1,0:T(8,128)}) custom-call(bf16[128,1024]{1,0:T(8,128)(2,1)} %rows_ref.1, bf16[128,1024]{1,0:T(8,128)(2,1)} %hidden_ref.1, f32[1024,128]{1,0:T(8,128)} %pad.8.clone.rw_ref, f32[128,1024]{1,0:T(8,128)} %pad_bitcast_fusion.rwt_ref, s32[8,128]{1,0:T(8,128)} %pad.9.ids_ref, ...), custom_call_target="tpu_custom_call" | custom-call | tf_op jit(solution)/shard_map/pallas_call | solution.py:310
  229.6 1.3 copy.16
  230.9 1.7 copy.19
Async XLA Ops:
  0.6 5.1 %copy-start.2 = (bf16[1,1,832,704]{2,3,1,0:T(8,128)(2,1)S(1)}, bf16[1,1,832,704]{2,3,1,0:T(8,128)(2,1)}, u32[]{:S(2)}) copy-start(bf16[1,1,832,704]{2,3,1,0:T(8,128)(2,1)} %param.13) | copy-start | bytes 3514372
  5.7 1.9 copy-start.3
  7.6 1.9 copy-start
  9.5 1.6 copy-start.1

commit v2 on v1

v2 whole, which is shorter than its diff:
```python
import jax
import jax.numpy as jnp
from jax import lax
from jax.experimental import pallas as pl
from jax.experimental.pallas import tpu as pltpu
from jax.sharding import Mesh
from jax.sharding import PartitionSpec as P

EXPERT = ("expert_0", "expert_1", "expert_2")
DP = ("dp_0", "dp_1")
DP_EXPERT = DP + EXPERT
PRECISE = lax.Precision.HIGHEST
F32 = jnp.float32
BF16 = jnp.bfloat16


def dot(a, b, dims=((1,), (0,)), precision=None):
    return lax.dot_general(a, b, (dims, ((), ())), preferred_element_type=F32, precision=precision)


def iota(shape, dim):
    return lax.broadcasted_iota(jnp.int32, shape, dim)


def kernel(
    rows_ref, hidden_ref, rw_ref, ids_ref, pre_gate_hbm, pre_up_hbm, wg_hbm, wu_hbm, wd_hbm,
    gx_ref, ru_ref,
    pre_gate, pre_up, wg, wu, wd, gathered, aux, aux_in, aux_relay,
    packed, arrived, back, returned, gate_out, gate_in, up_slope, act, act_up, probs,
    own_part, relay_part, comb_out, comb_mid, comb_in, pg_out, pg_early, pg_relay, pg_all,
    terms, x_in, slab_out, slab_in, tile_out, zl_in, zh_in, all_in, last_out, last_in,
    local_sem, row_ss, row_rs, aux_ss, aux_rs, go_ss, go_rs, ret_ss, ret_rs, gg_ss, gg_rs,
    comb_ss, comb_rs, pg_ss, pg_rs, zl_ss, zl_rs, x_ss, x_rs, slab_ss, slab_rs, zh_ss, zh_rs, all_ss, all_rs, last_ss, last_rs,
):
    zl, x = lax.axis_index("dp_0"), lax.axis_index("dp_1")
    zh, y, c = (lax.axis_index(a) for a in EXPERT)
    yc = y * 2 + c
    up_z, down_z, far_z = lax.rem(zh + 1, 4), lax.rem(zh + 3, 4), lax.rem(zh + 2, 4)
    origin = (zh, down_z, up_z, far_z)
    sent = []

    def at_z(z):
        return {"expert_0": z}

    def at_slab(place):
        return {"expert_1": place // 2, "expert_2": lax.rem(place, 2)}

    def copy(src, dst, ss, rs, to):
        return pltpu.make_async_remote_copy(
            src_ref=src, dst_ref=dst, send_sem=ss, recv_sem=rs,
            device_id=to, device_id_type=pl.DeviceIdType.MESH,
        )

    def send(*args):
        made = copy(*args)
        made.start()
        sent.append(made)
        return made

    local = [
        pltpu.make_async_copy(src, dst, local_sem.at[i])
        for i, (src, dst) in enumerate(
            ((pre_gate_hbm, pre_gate), (pre_up_hbm, pre_up), (wd_hbm, wd), (wg_hbm, wg), (wu_hbm, wu))
        )
    ]
    for made in local:
        made.start()
    barrier = pltpu.get_barrier_semaphore()
    meet = [at_z(up_z), at_z(down_z)]
    meet += [at_slab(lax.rem(yc + d, 8)) for d in range(1, 8)]
    meet += [{"dp_0": lax.rem(zl + d, 8)} for d in range(1, 8)]
    meet += [{"dp_1": lax.rem(x + d, 4)} for d in range(1, 4)]
    for to in meet:
        pl.semaphore_signal(barrier, inc=1, device_id=to, device_id_type=pl.DeviceIdType.MESH)

    logits = dot(rw_ref[...], hidden_ref[...].astype(F32), ((1,), (1,)), PRECISE)
    exponent = jnp.exp(logits)
    probability = exponent / jnp.sum(exponent, axis=0, keepdims=True)
    probs[...] = probability
    ids = ids_ref[...]
    expert = iota((32, 128), 0)
    chosen = jnp.zeros((32, 128), F32)
    for k in range(6):
        chosen += jnp.where(expert == ids[k : k + 1], 1.0, 0.0)
    r, t = iota((128, 128), 0), iota((128, 128), 1)
    earlier = jnp.where((r < t) & ((r >> 6) == (t >> 6)), 1.0, 0.0).astype(BF16)
    slot = jnp.where(chosen > 0.5, dot(chosen.astype(BF16), earlier), -1.0)
    for b in range(4):
        aux[b] = jnp.concatenate([slot[8 * b : 8 * b + 8], probability[8 * b : 8 * b + 8]], axis=0).astype(BF16)
    pl.semaphore_wait(barrier, len(meet))

    first, last = pl.ds(0, 64), pl.ds(64, 64)
    z_up, z_down = at_z(up_z), at_z(down_z)
    r1 = send(rows_ref.at[first], gathered.at[0, first], row_ss.at[0], row_rs.at[0], z_up)
    l1 = send(rows_ref.at[last], gathered.at[0, last], row_ss.at[1], row_rs.at[1], z_down)
    a_up = send(aux.at[up_z], aux_in.at[0], aux_ss.at[0], aux_rs.at[0], z_up)
    a_down = send(aux.at[down_z], aux_in.at[1], aux_ss.at[1], aux_rs.at[1], z_down)
    a_far = send(aux.at[far_z], aux_relay, aux_ss.at[2], aux_rs.at[2], z_up)
    r2 = send(rows_ref.at[last], gathered.at[1, last], row_ss.at[2], row_rs.at[2], z_up)
    l2 = send(rows_ref.at[first], gathered.at[1, first], row_ss.at[3], row_rs.at[3], z_down)

    def places(info):
        at = jnp.broadcast_to(info[:8].reshape(8, 1, 128), (8, 32, 128)).reshape(256, 128)
        r, t = iota((256, 128), 0), iota((256, 128), 1)
        hit = (at == (r & 15).astype(F32)) & (((r >> 4) & 1) == (t >> 6))
        return jnp.where(hit, 1.0, 0.0)

    def info_of(k):
        if k == 0:
            return aux[zh].astype(F32)
        if k == 3:
            return aux_in[2].astype(F32)
        return by_half(aux_in[k - 1].astype(F32), aux_in[2 - k].astype(F32))

    def by_half(a, b):
        return jnp.where(iota(a.shape, 1) < 64, a, b)

    def table_of(table, k):
        if k == 0 or k == 3:
            return table[origin[k]]
        return jnp.where((iota((256, 704), 0) & 16) == 0, table[origin[k]], table[origin[3 - k]])

    mine = pl.ds(pl.multiple_of(yc * 32, 32), 32)

    def slab_send(k, src, dst, ss, rs):
        dst[k, mine] = src[k, mine]
        for d in range(1, 8):
            place = lax.rem(yc + d, 8)
            theirs = pl.ds(pl.multiple_of(place * 32, 32), 32)
            send(src.at[k, theirs], dst.at[k, mine], ss.at[k, d], rs.at[k, d], at_slab(place))

    def slab_wait(k, src, dst, ss, rs):
        for d in range(1, 8):
            place = lax.rem(yc + 8 - d, 8)
            theirs = pl.ds(pl.multiple_of(place * 32, 32), 32)
            copy(src.at[k, theirs], dst.at[k, theirs], ss.at[k, d], rs.at[k, d], at_slab(place)).wait_recv()

    def dispatch(k):
        rows = rows_ref[...] if k == 0 else gathered[k - 1]
        packed[k] = dot(places(info_of(k)).astype(BF16), rows).astype(BF16)
        slab_send(k, packed, arrived, go_ss, go_rs)

    def run_expert(k):
        slab_wait(k, packed, arrived, go_ss, go_rs)
        dh = dot(arrived[k], wd[...], ((1,), (1,)))
        gate_grad = jnp.sum(dh * table_of(act_up, k), axis=1, keepdims=True)
        gate_out[k] = jnp.broadcast_to(gate_grad, (256, 128)).astype(BF16)
        slab_send(k, gate_out, gate_in, gg_ss, gg_rs)
        d_first = (dh * table_of(up_slope, k)).astype(BF16)
        d_second = (dh * table_of(act, k)).astype(BF16)
        back[k] = (dot(d_first, wg[...]) + dot(d_second, wu[...])).astype(BF16)
        slab_send(k, back, returned, ret_ss, ret_rs)

    def gate_part(k):
        slab_wait(k, gate_out, gate_in, gg_ss, gg_rs)
        gate_grad = places(info_of(k)) * gate_in[k].astype(F32)
        return jnp.sum(gate_grad.reshape(8, 32, 128), axis=1)

    def combine(k):
        info = info_of(k)
        gate = jnp.broadcast_to(info[8:].reshape(8, 1, 128), (8, 32, 128)).reshape(256, 128)
        weights = (places(info) * gate).T.astype(BF16)
        slab_wait(k, back, returned, ret_ss, ret_rs)
        return dot(weights, returned[k])

    dispatch(0)

    local[0].wait()
    local[1].wait()
    for o in range(4):
        saved_gate, saved_up = jnp.zeros((256, 704), F32), jnp.zeros((256, 704), F32)
        for n in range(2):
            start = n * 416 + o * 104
            lo = start // 128 * 128
            lanes = slice(lo, min(lo + 256, 832))
            r, s = iota((256, lanes.stop - lo), 0), iota((256, lanes.stop - lo), 1)
            real = (s == (r >> 5) * 13 + (r & 15) + (start - lo)) & ((r & 15) < 13) & (((r >> 4) & 1) == n)
            spread = jnp.where(real, 1.0, 0.0).astype(BF16)
            saved_gate += dot(spread, pre_gate[:, lanes], ((1,), (1,)))
            saved_up += dot(spread, pre_up[:, lanes], ((1,), (1,)))
        sg = 1.0 / (1.0 + jnp.exp(-saved_gate))
        active = saved_gate * sg
        act[o] = active
        act_up[o] = active * saved_up
        up_slope[o] = saved_up * (sg * (1.0 + saved_gate * (1.0 - sg)))
    for made in local[2:]:
        made.wait()
    run_expert(0)

    r1.wait_recv()
    r3 = send(gathered.at[0, first], gathered.at[2, first], row_ss.at[4], row_rs.at[4], z_up)
    l1.wait_recv()
    l3 = send(gathered.at[0, last], gathered.at[2, last], row_ss.at[5], row_rs.at[5], z_down)
    a_far.wait_recv()
    a_relay = send(aux_relay, aux_in.at[2], aux_ss.at[3], aux_rs.at[3], z_up)
    a_up.wait_recv()
    a_down.wait_recv()
    dispatch(1)
    pg_all[zh] = gate_part(0)
    own_part[...] = combine(0)
    run_expert(1)
    r2.wait_recv()
    l2.wait_recv()
    dispatch(2)
    pg_early[...] = gate_part(1)
    part = combine(1)
    comb_out[0] = part[:64].astype(BF16)
    c_down = send(comb_out.at[0], comb_in.at[1, 0], comb_ss.at[0], comb_rs.at[0], z_down)
    comb_out[1] = part[64:].astype(BF16)
    c_up = send(comb_out.at[1], comb_in.at[0, 1], comb_ss.at[1], comb_rs.at[1], z_up)
    run_expert(2)

    a_relay.wait_recv()
    r3.wait_recv()
    l3.wait_recv()
    dispatch(3)
    late, early = gate_part(2), pg_early[...]
    pg_out[0] = by_half(early, late)
    p_down = send(pg_out.at[0], pg_all.at[zh], pg_ss.at[0], pg_rs.at[0], z_down)
    pg_out[1] = by_half(late, early)
    p_up = send(pg_out.at[1], pg_all.at[zh], pg_ss.at[1], pg_rs.at[1], z_up)
    part = combine(2)
    relay_part[0] = part[:64]
    relay_part[1] = part[64:]
    run_expert(3)
    pg_out[2] = gate_part(3)
    p_far = send(pg_out.at[2], pg_relay, pg_ss.at[2], pg_rs.at[2], z_up)
    part = combine(3)
    comb_out[2] = part[:64].astype(BF16)
    comb_out[3] = part[64:].astype(BF16)

    def far_up(i):
        at = pl.ds(32 * i, 32)
        return send(comb_out.at[2, at], comb_mid.at[0, at], comb_ss.at[2 + i], comb_rs.at[2 + i], z_up)

    def far_down(i):
        at = pl.ds(32 * i, 32)
        return send(comb_out.at[3, at], comb_mid.at[1, at], comb_ss.at[4 + i], comb_rs.at[4 + i], z_down)

    def joined_up(i):
        at = pl.ds(32 * i, 32)
        comb_out[4, at] = (relay_part[0, at] + comb_mid[0, at].astype(F32)).astype(BF16)
        return send(comb_out.at[4, at], comb_in.at[0, 0, at], comb_ss.at[6 + i], comb_rs.at[6 + i], z_up)

    def joined_down(i):
        at = pl.ds(32 * i, 32)
        comb_out[5, at] = (relay_part[1, at] + comb_mid[1, at].astype(F32)).astype(BF16)
        return send(comb_out.at[5, at], comb_in.at[1, 1, at], comb_ss.at[8 + i], comb_rs.at[8 + i], z_down)

    f1_down = far_down(0)
    p_far.wait_recv()
    p_relay = send(pg_relay, pg_all.at[down_z], pg_ss.at[3], pg_rs.at[3], z_up)
    f1_up = far_up(0)
    f2_down = far_down(1)
    f2_up = far_up(1)

    p_down.wait_recv()
    p_up.wait_recv()
    p_relay.wait_recv()
    probability = probs[...]
    prob_grad = pg_all[...].reshape(32, 128)
    logit_grad = probability * (prob_grad - jnp.sum(probability * prob_grad, axis=0, keepdims=True))
    term = dot(logit_grad, hidden_ref[...].astype(F32), precision=PRECISE)
    for i in range(8):
        terms[i // 2, 32 * (i % 2) : 32 * (i % 2) + 32] = term[:, 128 * i : 128 * i + 128]

    def share(src, dst, ss, rs, me, count, to):
        made = []
        for d in range(1, count):
            place = lax.rem(me + d, count)
            made.append(send(src(place), dst.at[me], ss.at[d], rs.at[d], to(place)))
        return made

    def gather(src, dst, ss, rs, me, count, to):
        for d in range(1, count):
            place = lax.rem(me + count - d, count)
            copy(src(place), dst.at[place], ss.at[d], rs.at[d], to(place)).wait_recv()

    def zl_at(place):
        return {"dp_0": place}

    def x_at(place):
        return {"dp_1": place}

    x_args = (lambda place: terms.at[place], x_in, x_ss, x_rs, x, 4, x_at)
    slab_args = (lambda place: slab_out.at[place], slab_in, slab_ss, slab_rs, yc, 8, at_slab)
    zl_args = (lambda place: tile_out.at[0], zl_in, zl_ss, zl_rs, zl, 8, zl_at)
    all_args = (lambda place: tile_out.at[3], all_in, all_ss, all_rs, yc, 8, at_slab)
    last_args = (lambda place: last_out, last_in, last_ss, last_rs, x, 4, x_at)
    x_in[x] = terms[x]
    share(*x_args)
    turned = jnp.concatenate([logit_grad, jnp.zeros((96, 128), F32)], axis=0).T
    own_part[...] += dot(turned[:, :32], rw_ref[...], precision=PRECISE)
    gather(*x_args)
    slab_out[...] = jnp.sum(x_in[...], axis=0).reshape(8, 8, 128)
    slab_in[yc] = slab_out[yc]
    share(*slab_args)
    gather(*slab_args)
    tile = jnp.sum(slab_in[...], axis=0)
    tile_out[0] = tile
    zl_in[zl] = tile
    share(*zl_args)

    f1_up.wait_recv()
    e1_up = joined_up(0)
    f1_down.wait_recv()
    e1_down = joined_down(0)
    gather(*zl_args)
    tile = jnp.sum(zl_in[...], axis=0)
    tile_out[1] = tile
    h1 = send(tile_out.at[1], zh_in.at[0], zh_ss.at[0], zh_rs.at[0], at_z(zh + 1 - 2 * lax.rem(zh, 2)))
    f2_up.wait_recv()
    e2_up = joined_up(1)
    f2_down.wait_recv()
    e2_down = joined_down(1)
    h1.wait_recv()
    tile = tile + zh_in[0]
    tile_out[2] = tile
    h2 = send(tile_out.at[2], zh_in.at[1], zh_ss.at[1], zh_rs.at[1], at_z(3 - zh))
    h2.wait_recv()
    tile = tile + zh_in[1]
    tile_out[3] = tile
    all_in[yc] = tile
    share(*all_args)
    gather(*all_args)
    tiles = jnp.sum(all_in[...] * all_in[...], axis=0)
    square = jnp.sum(jnp.sum(tiles, axis=1, keepdims=True), axis=0, keepdims=True)
    last_out[:8] = all_in[lax.rem(zl, 2) * 4 + zh]
    last_out[8:] = jnp.broadcast_to(square, (8, 128))
    last_in[x] = last_out[...]
    share(*last_args)

    for made in (c_down, c_up, e1_up, e1_down, e2_up, e2_down):
        made.wait_recv()
    for half in range(2):
        at = pl.ds(64 * half, 64)
        both = comb_in[0, half].astype(F32) + comb_in[1, half].astype(F32)
        gx_ref[at] = (own_part[at] + both).astype(BF16)

    gather(*last_args)
    tile = last_in[zl // 2][:8]
    column = jnp.where(iota((8, 128), 0) == yc, tile, 0.0)
    column = jnp.sum(column, axis=0, keepdims=True)
    column = sum(jnp.where(x == i, column[:, 32 * i : 32 * i + 32], 0.0) for i in range(4))
    square = jnp.sum(last_in[...], axis=0)[8:9, :1]
    ru_ref[...] = column * jnp.minimum(1.0, jnp.sqrt(1024 * 32 / (square + 1e-06)))
    for made in sent:
        made.wait_send()


def local(hidden, grad_out, router_weight, expert_ids, pre_gate, pre_up, w_gate, w_up, w_down):
    vmem, dma = pltpu.VMEM, pltpu.SemaphoreType.DMA
    in_vmem, in_hbm = pl.BlockSpec(memory_space=pltpu.VMEM), pl.BlockSpec(memory_space=pl.ANY)
    grad_x, update = pl.pallas_call(
        kernel,
        out_shape=(jax.ShapeDtypeStruct((128, 1024), BF16), jax.ShapeDtypeStruct((1, 32), F32)),
        in_specs=[in_vmem] * 4 + [in_hbm] * 5,
        out_specs=(in_vmem, in_vmem),
        scratch_shapes=[
            vmem((704, 832), BF16), vmem((704, 832), BF16),
            vmem((704, 1024), BF16), vmem((704, 1024), BF16), vmem((704, 1024), BF16),
            vmem((3, 128, 1024), BF16), vmem((4, 16, 128), BF16), vmem((3, 16, 128), BF16), vmem((16, 128), BF16),
            vmem((4, 256, 1024), BF16), vmem((4, 256, 1024), BF16), vmem((4, 256, 1024), BF16), vmem((4, 256, 1024), BF16),
            vmem((4, 256, 128), BF16), vmem((4, 256, 128), BF16),
            vmem((4, 256, 704), F32), vmem((4, 256, 704), F32), vmem((4, 256, 704), F32), vmem((32, 128), F32),
            vmem((128, 1024), F32), vmem((2, 64, 1024), F32), vmem((6, 64, 1024), BF16), vmem((2, 64, 1024), BF16),
            vmem((2, 2, 64, 1024), BF16), vmem((3, 8, 128), F32), vmem((8, 128), F32), vmem((8, 128), F32), vmem((4, 8, 128), F32),
            vmem((4, 64, 128), F32), vmem((4, 64, 128), F32), vmem((8, 8, 128), F32), vmem((8, 8, 128), F32),
            vmem((4, 8, 128), F32), vmem((8, 8, 128), F32), vmem((2, 8, 128), F32), vmem((8, 8, 128), F32),
            vmem((16, 128), F32), vmem((4, 16, 128), F32),
            dma((5,)), dma((6,)), dma((6,)), dma((4,)), dma((4,)), dma((4, 8)), dma((4, 8)), dma((4, 8)), dma((4, 8)),
            dma((4, 8)), dma((4, 8)), dma((10,)), dma((10,)), dma((4,)), dma((4,)), dma((8,)), dma((8,)), dma((4,)), dma((4,)), dma((8,)), dma((8,)),
            dma((2,)), dma((2,)), dma((8,)), dma((8,)), dma((4,)), dma((4,)),
        ],
        compiler_params=pltpu.CompilerParams(collective_id=0, has_side_effects=True),
    )(
        grad_out, hidden, router_weight.T, expert_ids.T,
        pre_gate[0, 0].T, pre_up[0, 0].T, w_gate[0].T, w_up[0].T, w_down[0],
    )
    return grad_x, update.reshape(32, 1)


def solution(mesh):
    torus = Mesh(mesh.devices.reshape(8, 4, 4, 4, 2), DP_EXPERT)
    return jax.shard_map(
        local,
        mesh=torus,
        in_specs=(
            P(DP_EXPERT, None),
            P(DP_EXPERT, None),
            P(),
            P(DP_EXPERT, None),
            P(DP, EXPERT, None, None),
            P(DP, EXPERT, None, None),
            P(EXPERT, None, None),
            P(EXPERT, None, None),
            P(EXPERT, None, None),
        ),
        out_specs=(P(DP_EXPERT, None), P(DP, EXPERT)),
        check_vma=False,
    )
```

time: 233 us -> 204 us (0.88)
  the two profiles are of different devices: /device:TPU:1 before, /device:TPU:96 now
where the time goes in v2:
time: 204 us
  Pallas kernels  200 us (98%)
  local copies, waits for them, and re-layouts  2.8 us (1%)
    pallas_call x1, Pallas kernels, local(): pl.pallas_call(kernel, out_shape=(jax.ShapeDtypeStruct((128, 1024), BF16)...  200 us

profile of v2, /device:TPU:96, one launch (start us, length us, event | category | flops | bytes accessed | tf_op | source)
XLA Modules:
  0.0 203.7 jit_solution(7602127815265537758)
XLA Ops:
  0.6 200.2 %shard_map.104 = (bf16[128,1024]{1,0:T(8,128)(2,1)}, f32[1,32]{1,0:T(1,128)}) custom-call(bf16[128,1024]{1,0:T(8,128)(2,1)} %rows_ref.1, bf16[128,1024]{1,0:T(8,128)(2,1)} %hidden_ref.1, f32[32,1024]{1,0:T(8,128)} %bitcast.21, s32[6,128]{1,0:T(8,128)} %bitcast.22, bf16[704,832]{1,0:T(8,128)(2,1)} %bitcast.19, bf16[704,832]{1,0:T(8,128)(2,1)} %bitcast.20, ...), custom_call_target="tpu_custom_call" | custom-call | tf_op jit(solution)/shard_map/pallas_call | solution.py:354
  200.9 1.7 copy.13
  202.5 1.1 copy.14
